TPU v7x, 128 devices: a whole 4x4x4 slice. The times are simulated.
128 devices in a mesh: head: 4 (over z_hi, core), seq: 32 (over y, x, z_lo).
Axes of the slice: x: 4, y: 4, z: 4 (z_hi: 2, z_lo: 2; z = z_hi * 2 + z_lo), core: 2. Of those that a mesh axis runs over, the one named last changes fastest.
Arguments:
- skip_stream: bfloat16 [4096, 4096], P('head', 'seq'), may hold values from -6 to 6
- acceptance_vector: bfloat16 [4096, 4096], P('head', 'seq'), may hold values from -6 to 6
- address_vectors: bfloat16 [4096, 4096], P('head', 'seq'), may hold values from -0.75 to 0.75
- content_vectors: bfloat16 [4096, 4096], P('head', 'seq'), may hold values from -6 to 6
- emission_valve: bfloat16 [4096, 4096], P('head', 'seq'), may hold values from -6 to 6
- fading_exponent: bfloat16 [4096, 4096], P('head', 'seq'), may hold values from -0.7 to 0
- adaptation_speed: bfloat16 [4096, 4096], P('head', 'seq'), may hold values from 0 to 0.9
- erasure_factor: float32 [4096], P('head'), may hold values from 0.3 to 3
- reward_coefficient: float32 [4096], P('head'), may hold values from -4 to 4
- cluster_multiplier: float32 [4096], P('head'), may hold values from 0.5 to 2
- cluster_offset: float32 [4096], P('head'), may hold values from -3 to 3
- projection_weights: bfloat16 [4096, 4096], P(None, 'head'), may hold values from -0.125 to 0.125
Outputs:
- layer_output: bfloat16 [4096, 4096], P('head', 'seq')
All inputs are finite; a program needn't handle non-finite values.
Results may differ from a plain program's by a relative error of at most 0.0048.
Values may be sent and summed in bfloat16 or wider, within the bound.
A program may use at most 128 MiB of HBM per device.

v0:
```python
import functools
import jax
import jax.numpy as jnp
from jax import lax
from jax.experimental import pallas as pl
from jax.experimental.pallas import tpu as pltpu
from jax.sharding import PartitionSpec as P

MESH = pl.DeviceIdType.MESH
CH = 64
HEADS = 16
TOK = 128
SLABS = 32
ROWS = 1024
EXTRA = 16
GROUP = 8
BATCH = 8
CHUNK = 256
F32 = jnp.float32
BF16 = jnp.bfloat16


def dot(left, right, dims=((1,), (0,)), precision=lax.Precision.HIGH):
    return lax.dot_general(
        left, right, (dims, ((), ())), precision=precision, preferred_element_type=F32
    )


def halves(x):
    high = x.astype(BF16)
    return high, (x - high.astype(F32)).astype(BF16)


def fold(x):
    return x[:, :TOK] + x[:, TOK:]


def mm(left, right):
    return jnp.dot(left, right, preferred_element_type=F32)


def kernel(
    skip_ref, r_ref, k_ref, v_ref, g_ref, w_ref, a_ref, ef_ref, rc_ref, gm_ref, gb_ref, wt_hbm,
    out_ref,
    par, comb, read, local, inbox, prefix, outbox, entering, mixed, weights,
    send_a, got_a, held_b, send_b, got_b, total,
    masks, pull_t, key_t, ends_t, ahead_s, pair_s, pread_s, kread_s, inv_s, inv, part_s, seen_s,
    recv_s, decay_s, solved_s, rest,
    wt_sem, comb_send, comb_recv, state_send, state_recv, rs_send, rs_recv,
):
    head = lax.axis_index("head")
    me = lax.axis_index("seq")
    core = lax.rem(head, 2)
    pair = head // 2

    def owner_of(h):
        odd, place = h // 8, h % 8
        y = place // 2
        x = 2 * (place % 2) + (y + odd) % 2
        return y * 8 + x * 2 + (odd + core) % 2

    barrier = pltpu.get_barrier_semaphore()

    def greet(d, carry):
        pl.semaphore_signal(
            barrier, inc=1, device_id=(head, lax.rem(me + d, SLABS)), device_id_type=MESH
        )
        return carry

    lax.fori_loop(1, SLABS, greet, 0)

    def greet_head(d, carry):
        pl.semaphore_signal(
            barrier, inc=1, device_id=(lax.rem(head + d, 4), me), device_id_type=MESH
        )
        return carry

    lax.fori_loop(1, 4, greet_head, 0)
    wt_copy = pltpu.make_async_copy(wt_hbm, weights, wt_sem)
    wt_copy.start()

    def spread(p, ref):
        for j in range(8):
            par[p, j * 128 : (j + 1) * 128, :] = jnp.broadcast_to(ref[j : j + 1, :], (128, 128)).T

    spread(0, ef_ref)

    row = lax.broadcasted_iota(jnp.int32, (TOK, TOK), 0)
    col = lax.broadcasted_iota(jnp.int32, (TOK, TOK), 1)
    upto = jnp.where(row <= col, 1.0, 0.0).astype(BF16)
    for level in range(7):
        masks[level] = jnp.where(((row ^ col) >> level) == 1, 1.0, 0.0).astype(BF16)
    zero = jnp.zeros((TOK, TOK), BF16)
    diag = lax.broadcasted_iota(jnp.int32, (CH, TOK), 0) == lax.broadcasted_iota(
        jnp.int32, (CH, TOK), 1
    )
    left_half = lax.broadcasted_iota(jnp.int32, (CH, TOK), 1) < CH

    def wide(pair):
        return jnp.concatenate(
            [
                jnp.concatenate([pair[:, :TOK], pair[:, TOK:]], axis=1),
                jnp.concatenate([pair[:, :TOK], zero], axis=1),
            ],
            axis=0,
        )

    def beside(x):
        return jnp.concatenate(halves(x), axis=1)

    def turned(x):
        return jnp.concatenate(halves(x), axis=0).T

    def group_local(base):
        for i in range(BATCH):
            rows = slice((base + i) * CH, (base + i + 1) * CH)
            w16 = w_ref[rows, :]
            running = mm(w16, upto)
            kf = k_ref[rows, :].astype(F32)
            scaled = kf * par[0, rows, :]
            removal = scaled * lax.rsqrt(jnp.sum(scaled * scaled, axis=0, keepdims=True) + 1e-6)
            pulled = removal * a_ref[rows, :].astype(F32)
            mid = running[:, 63:64]
            end = running[:, 127:128]
            back = jnp.exp(mid - running)
            at_mid = jnp.exp(mid)
            to_end = back * jnp.exp(end - mid)
            removal_fwd = -removal * jnp.exp(running - w16.astype(F32) - mid)
            recept_fwd = r_ref[rows, :].astype(F32) * jnp.exp(running - mid)
            pull_t[i] = turned(pulled * back)
            key_t[i] = turned(kf * back)
            ends_t[i, :, :TOK] = turned(pulled * to_end)
            ends_t[i, :, TOK:] = turned(kf * to_end)
            rem_hi, rem_lo = halves(removal_fwd)
            rec_hi, rec_lo = halves(recept_fwd)
            ahead_s[i, :CH, :TOK] = rem_hi
            ahead_s[i, CH:, :TOK] = rem_lo
            ahead_s[i, :CH, TOK:] = rec_hi
            ahead_s[i, CH:, TOK:] = rec_lo
            seen_s[i, CH:, :] = removal_fwd * at_mid
            recv_s[base + i] = recept_fwd * at_mid
            decay_s[i] = jnp.where(diag, jnp.exp(end), 0.0)
        for i in range(BATCH):
            ahead = ahead_s[i]
            ahead = jnp.concatenate([ahead[:CH], ahead[:CH], ahead[CH:], ahead[CH:]], axis=0)
            pull = pull_t[i]
            from_pull = mm(jnp.concatenate([pull, pull], axis=1), ahead)
            pair_mix = jnp.where(row < col, from_pull[:, :TOK], 0.0)
            pair_s[i] = beside(pair_mix)
            start = jnp.where(row == col, 1.0, pair_mix * masks[0].astype(F32))
            inv[i] = start
            inv_s[i] = beside(start)
            pread_s[base + i] = from_pull[:, TOK:]
            key = key_t[i]
            from_key = mm(jnp.concatenate([key, key], axis=1), ahead)
            kread_s[base + i] = from_key[:, TOK:]
            part_s[i] = beside(jnp.where(row < col, from_key[:, :TOK], 0.0))
        for i in range(BATCH):
            rows = slice((base + i) * CH, (base + i + 1) * CH)
            seen_s[i, :CH, :] = fold(mm(v_ref[rows, :], part_s[i]))
        for level in range(1, 7):
            mask = masks[level]
            for i in range(BATCH):
                off = pair_s[i] * jnp.concatenate([mask, mask], axis=1)
                part_s[i] = beside(fold(mm(inv_s[i], wide(off))))
            for i in range(BATCH):
                new = inv[i] + fold(mm(part_s[i], wide(inv_s[i])))
                if level < 6:
                    inv[i] = new
                inv_s[i] = beside(new)
        for i in range(BATCH):
            solved_s[base + i] = beside(fold(mm(beside(seen_s[i]), wide(inv_s[i]))))
        for i in range(BATCH):
            h = base + i
            rows = slice(h * CH, (h + 1) * CH)
            pull_end = ends_t[i, :, :TOK]
            ops = mm(solved_s[h], jnp.concatenate([pull_end, pull_end], axis=0))
            state = ops[:CH] + mm(v_ref[rows, :], ends_t[i, :, TOK:])
            trans = ops[CH:]
            state = state + pltpu.roll(state, CH, 1)
            trans = trans + pltpu.roll(trans, CH, 1) + decay_s[i]
            sent = jnp.where(left_half, trans, state).astype(BF16)
            comb[h, :CH, :] = sent
            missed = jnp.where(diag, trans - sent.astype(F32), 0.0)
            comb[h, CH:, :] = jnp.broadcast_to(
                jnp.sum(missed, axis=0, keepdims=True), (EXTRA, TOK)
            ).astype(BF16)

    def group_read(base):
        for i in range(BATCH):
            h = base + i
            rows = slice(h * CH, (h + 1) * CH)
            pread = beside(jnp.where(row <= col, pread_s[h], 0.0))
            kread = beside(jnp.where(row <= col, kread_s[h], 0.0))
            out = fold(mm(solved_s[h], wide(pread)))
            local[h] = out[:CH] + fold(mm(v_ref[rows, :], kread))
            read[h] = jnp.concatenate(halves(out[CH:] + recv_s[h]), axis=0)
            kf = k_ref[rows, :].astype(F32)
            vf = v_ref[rows, :].astype(F32)
            rf = r_ref[rows, :].astype(F32)
            bonus = jnp.sum(rf * kf * par[1, rows, :], axis=0, keepdims=True) * vf
            rest[h] = bonus + par[3, rows, :]

    def comb_copy(h):
        return pltpu.make_async_remote_copy(
            src_ref=comb.at[h],
            dst_ref=inbox.at[me],
            send_sem=comb_send.at[h],
            recv_sem=comb_recv.at[me],
            device_id=(head, owner_of(h)),
            device_id_type=MESH,
        )

    def send_comb(t, carry):
        h = (t // BATCH) * BATCH + (t + me + 3 * (me // 8)) % BATCH

        @pl.when(owner_of(h) != me)
        def _():
            comb_copy(h).start()

        @pl.when(owner_of(h) == me)
        def _():
            inbox[me] = comb[h]

        return carry

    for base in range(0, HEADS, BATCH):
        group_local(base)
        if base == 0:
            pl.semaphore_wait(barrier, SLABS - 1 + 3)
        lax.fori_loop(base, base + BATCH, send_comb, 0)
    spread(1, rc_ref)
    spread(2, gm_ref)
    spread(3, gb_ref)
    for base in range(0, HEADS, BATCH):
        group_read(base)

    my_y, my_x = me // 8, (me // 2) % 4
    my_head = ((my_x + my_y) % 2) * 8 + 2 * my_y + my_x // 2

    def state_copy(i):
        return pltpu.make_async_remote_copy(
            src_ref=outbox.at[i],
            dst_ref=entering.at[my_head],
            send_sem=state_send.at[i],
            recv_sem=state_recv.at[my_head],
            device_id=(head, i),
            device_id_type=MESH,
        )

    @pl.when(owner_of(my_head) == me)
    def _():
        def arrive(d, carry):
            i = lax.rem(me + d, SLABS)
            pltpu.make_async_remote_copy(
                src_ref=comb.at[0],
                dst_ref=inbox.at[i],
                send_sem=comb_send.at[0],
                recv_sem=comb_recv.at[i],
                device_id=(head, i),
                device_id_type=MESH,
            ).wait_recv()
            return carry

        lax.fori_loop(1, SLABS, arrive, 0)

        def pack(i, value):
            value = value.astype(BF16)
            outbox[i] = jnp.concatenate([value[: CH // 2], value[CH // 2 :]], axis=1)

        def item_of(i):
            item = inbox[i]
            trans = item[:CH, :CH]
            state = pltpu.roll(item[:CH].astype(F32), CH, 1)[:, :CH]
            return trans, item[CH : CH + 1, :CH].astype(F32), state

        groups = SLABS // GROUP
        for g in range(groups):
            trans, missed, state = item_of(g * GROUP)
            whole = trans.astype(F32) + jnp.where(diag[:, :CH], missed, 0.0)
            prefix[g * GROUP] = jnp.concatenate([state, whole], axis=0)

        def step(i, carry):
            for g in range(groups):
                trans, missed, state = item_of(g * GROUP + i)
                old = prefix[g * GROUP + i - 1]
                high, low = halves(old)
                moved = mm(high, trans) + mm(low, trans) + old * missed
                prefix[g * GROUP + i, :CH, :] = moved[:CH] + state
                prefix[g * GROUP + i, CH:, :] = moved[CH:]
            return carry

        lax.fori_loop(1, GROUP, step, 0)
        start = jnp.zeros((CH, CH), F32)
        starts = [start]
        for g in range(groups - 1):
            done = prefix[g * GROUP + GROUP - 1]
            start = dot(start, done[CH:]) + done[:CH]
            starts.append(start)
        for g in range(groups):
            pack(g * GROUP, starts[g])
            for i in range(1, GROUP):
                done = prefix[g * GROUP + i - 1]
                pack(g * GROUP + i, dot(starts[g], done[CH:]) + done[:CH])

        def give(d, carry):
            state_copy(lax.rem(me + d, SLABS)).start()
            return carry

        lax.fori_loop(1, SLABS, give, 0)
        entering[my_head] = outbox[me]

    def arrived(h):
        @pl.when(owner_of(h) != me)
        def _():
            pltpu.make_async_remote_copy(
                src_ref=outbox.at[0],
                dst_ref=entering.at[h],
                send_sem=state_send.at[0],
                recv_sem=state_recv.at[h],
                device_id=(head, owner_of(h)),
                device_id_type=MESH,
            ).wait_recv()

    for base in range(0, HEADS, BATCH):
        for i in range(BATCH):
            arrived(base + i)
        outs = []
        for i in range(BATCH):
            reading = read[base + i]
            state = entering[base + i]
            nil = jnp.zeros((CH, TOK), BF16)
            upper = jnp.concatenate([reading[:CH], nil, reading[CH:], nil], axis=0)
            lower = jnp.concatenate([nil, reading[:CH], nil, reading[CH:]], axis=0)
            y = mm(
                jnp.concatenate([state, state], axis=1),
                jnp.concatenate([upper, lower], axis=1),
            )
            outs.append(jnp.concatenate([y[:, :TOK], y[:, TOK:]], axis=0) + local[base + i])
        for i in range(BATCH):
            rows = slice((base + i) * CH, (base + i + 1) * CH)
            y = outs[i]
            centred = y - jnp.mean(y, axis=0, keepdims=True)
            spreading = jnp.mean(centred * centred, axis=0, keepdims=True)
            normed = centred * lax.rsqrt(spreading + 0.00064) * par[2, rows, :]
            mixed[rows, :] = ((normed + rest[base + i]) * g_ref[rows, :].astype(F32)).astype(BF16)

    wt_copy.wait()
    partner = pair * 2 + 1 - core
    across = (1 - pair) * 2 + core

    def piece(dest, c):
        rows = pl.ds(pl.multiple_of(dest * ROWS + c * CHUNK, CHUNK), CHUNK)
        return dot(weights[rows, :], mixed[...], precision=None)

    pieces = ROWS // CHUNK

    def near_copy(c):
        return pltpu.make_async_remote_copy(
            src_ref=send_a.at[c],
            dst_ref=got_a.at[c],
            send_sem=rs_send.at[c],
            recv_sem=rs_recv.at[c],
            device_id=(partner, me),
            device_id_type=MESH,
        )

    def far_copy(c):
        return pltpu.make_async_remote_copy(
            src_ref=send_b.at[c],
            dst_ref=got_b.at[c],
            send_sem=rs_send.at[2 * pieces + c],
            recv_sem=rs_recv.at[2 * pieces + c],
            device_id=(across, me),
            device_id_type=MESH,
        )

    for c in range(pieces):
        send_a[c] = piece((1 - pair) * 2 + 1 - core, c)
        near_copy(c).start()
    for c in range(pieces):
        held_b[c] = piece(across, c)
        near_copy(c).wait_recv()
        send_b[c] = (held_b[c] + got_a[c]).astype(BF16)
        far_copy(c).start()
    for c in range(pieces):
        send_a[pieces + c] = piece(partner, c)
        near_copy(pieces + c).start()
    for c in range(pieces):
        rows = slice(c * CHUNK, (c + 1) * CHUNK)
        total[rows, :] = piece(head, c) + skip_ref[rows, :].astype(F32)
        near_copy(pieces + c).wait_recv()
        total[rows, :] = total[rows, :] + got_a[pieces + c]
    for c in range(pieces):
        rows = slice(c * CHUNK, (c + 1) * CHUNK)
        far_copy(c).wait_recv()
        out_ref[rows, :] = (total[rows, :] + got_b[c].astype(F32)).astype(BF16)

    for c in range(2 * pieces):
        near_copy(c).wait_send()
    for c in range(pieces):
        far_copy(c).wait_send()

    def sent_comb(h, carry):
        @pl.when(owner_of(h) != me)
        def _():
            comb_copy(h).wait_send()

        return carry

    lax.fori_loop(0, HEADS, sent_comb, 0)

    @pl.when(owner_of(my_head) == me)
    def _():
        def sent_state(d, carry):
            state_copy(lax.rem(me + d, SLABS)).wait_send()
            return carry

        lax.fori_loop(1, SLABS, sent_state, 0)


def on_device(skip, r, k, v, g, w, a, ef, rc, gm, gb, wt):
    vmem = pl.BlockSpec(memory_space=pltpu.VMEM)
    pieces = ROWS // CHUNK
    dma = pltpu.SemaphoreType.DMA
    return pl.pallas_call(
        kernel,
        out_shape=jax.ShapeDtypeStruct((ROWS, TOK), BF16),
        in_specs=[vmem] * 11 + [pl.BlockSpec(memory_space=pl.ANY)],
        out_specs=vmem,
        scratch_shapes=[
            pltpu.VMEM((4, ROWS, TOK), F32),
            pltpu.VMEM((HEADS, CH + EXTRA, 2 * CH), BF16),
            pltpu.VMEM((HEADS, 2 * CH, TOK), BF16),
            pltpu.VMEM((HEADS, CH, TOK), F32),
            pltpu.VMEM((SLABS, CH + EXTRA, 2 * CH), BF16),
            pltpu.VMEM((SLABS, 2 * CH, CH), F32),
            pltpu.VMEM((SLABS, CH // 2, 2 * CH), BF16),
            pltpu.VMEM((HEADS, CH // 2, 2 * CH), BF16),
            pltpu.VMEM((ROWS, TOK), BF16),
            pltpu.VMEM((4 * ROWS, ROWS), BF16),
            pltpu.VMEM((2 * pieces, CHUNK, TOK), F32),
            pltpu.VMEM((2 * pieces, CHUNK, TOK), F32),
            pltpu.VMEM((pieces, CHUNK, TOK), F32),
            pltpu.VMEM((pieces, CHUNK, TOK), BF16),
            pltpu.VMEM((pieces, CHUNK, TOK), BF16),
            pltpu.VMEM((ROWS, TOK), F32),
            pltpu.VMEM((7, TOK, TOK), BF16),
            pltpu.VMEM((BATCH, TOK, TOK), BF16),
            pltpu.VMEM((BATCH, TOK, TOK), BF16),
            pltpu.VMEM((BATCH, TOK, 2 * TOK), BF16),
            pltpu.VMEM((BATCH, TOK, 2 * TOK), BF16),
            pltpu.VMEM((BATCH, TOK, 2 * TOK), BF16),
            pltpu.VMEM((HEADS, TOK, TOK), F32),
            pltpu.VMEM((HEADS, TOK, TOK), F32),
            pltpu.VMEM((BATCH, TOK, 2 * TOK), BF16),
            pltpu.VMEM((BATCH, TOK, TOK), F32),
            pltpu.VMEM((BATCH, TOK, 2 * TOK), BF16),
            pltpu.VMEM((BATCH, TOK, TOK), F32),
            pltpu.VMEM((HEADS, CH, TOK), F32),
            pltpu.VMEM((BATCH, CH, TOK), F32),
            pltpu.VMEM((HEADS, TOK, 2 * TOK), BF16),
            pltpu.VMEM((HEADS, CH, TOK), F32),
            dma(()),
            dma((HEADS,)),
            dma((SLABS,)),
            dma((SLABS,)),
            dma((HEADS,)),
            dma((3 * pieces,)),
            dma((3 * pieces,)),
        ],
        compiler_params=pltpu.CompilerParams(
            collective_id=0, has_side_effects=True, vmem_limit_bytes=40 * 1024 * 1024
        ),
    )(skip, r, k, v, g, w, a, *(p.reshape(8, 128) for p in (ef, rc, gm, gb)), wt)


def solution(mesh):
    split = P("head", "seq")
    vec = P("head")
    return jax.shard_map(
        on_device,
        mesh=mesh,
        in_specs=(split,) * 7 + (vec,) * 4 + (P(None, "head"),),
        out_specs=split,
        check_vma=False,
    )
```

profile of v0, /device:TPU:1, one launch (start us, length us, event | category | flops | bytes accessed | tf_op | source)
XLA Modules:
  0.0 52.7 jit_solution(5121564896542191987)
XLA Ops:
  0.0 0.0 copy-start
  0.0 3.4 %copy-done = bf16[4096,1024]{1,0:T(8,128)(2,1)S(1)} copy-done((bf16[4096,1024]{1,0:T(8,128)(2,1)S(1)}, bf16[4096,1024]{1,0:T(8,128)(2,1)}, u32[]{:S(2)}) %copy-start) | copy-done | bytes 8388632
  3.4 0.0 copy-start.1
  3.4 0.9 %copy-done.1 = bf16[1024,128]{1,0:T(8,128)(2,1)S(1)} copy-done((bf16[1024,128]{1,0:T(8,128)(2,1)S(1)}, bf16[1024,128]{1,0:T(8,128)(2,1)}, u32[]{:S(2)}) %copy-start.1) | copy-done | bytes 262168
  4.3 0.0 copy-start.2
  4.3 0.9 %copy-done.2 = bf16[1024,128]{1,0:T(8,128)(2,1)S(1)} copy-done((bf16[1024,128]{1,0:T(8,128)(2,1)S(1)}, bf16[1024,128]{1,0:T(8,128)(2,1)}, u32[]{:S(2)}) %copy-start.2) | copy-done | bytes 262168
  5.3 0.0 copy-start.3
  5.3 0.9 %copy-done.3 = bf16[1024,128]{1,0:T(8,128)(2,1)S(1)} copy-done((bf16[1024,128]{1,0:T(8,128)(2,1)S(1)}, bf16[1024,128]{1,0:T(8,128)(2,1)}, u32[]{:S(2)}) %copy-start.3) | copy-done | bytes 262168
  6.2 0.0 copy-start.4
  6.2 0.9 %copy-done.4 = bf16[1024,128]{1,0:T(8,128)(2,1)S(1)} copy-done((bf16[1024,128]{1,0:T(8,128)(2,1)S(1)}, bf16[1024,128]{1,0:T(8,128)(2,1)}, u32[]{:S(2)}) %copy-start.4) | copy-done | bytes 262168
  7.2 0.0 copy-start.5
  7.2 0.9 %copy-done.5 = bf16[1024,128]{1,0:T(8,128)(2,1)S(1)} copy-done((bf16[1024,128]{1,0:T(8,128)(2,1)S(1)}, bf16[1024,128]{1,0:T(8,128)(2,1)}, u32[]{:S(2)}) %copy-start.5) | copy-done | bytes 262168
  8.1 0.0 copy-start.6
  8.1 0.9 %copy-done.6 = bf16[1024,128]{1,0:T(8,128)(2,1)S(1)} copy-done((bf16[1024,128]{1,0:T(8,128)(2,1)S(1)}, bf16[1024,128]{1,0:T(8,128)(2,1)}, u32[]{:S(2)}) %copy-start.6) | copy-done | bytes 262168
  9.1 0.0 copy-start.7
  9.1 0.9 %copy-done.7 = bf16[1024,128]{1,0:T(8,128)(2,1)S(1)} copy-done((bf16[1024,128]{1,0:T(8,128)(2,1)S(1)}, bf16[1024,128]{1,0:T(8,128)(2,1)}, u32[]{:S(2)}) %copy-start.7) | copy-done | bytes 262168
  10.0 0.0 copy-start.8
  10.0 0.7 %copy-done.8 = f32[1024]{0:T(1024)S(1)} copy-done((f32[1024]{0:T(1024)S(1)}, f32[1024]{0:T(1024)}, u32[]{:S(2)}) %copy-start.8) | copy-done | bytes 4120
  10.7 0.0 copy-start.9
  10.7 0.7 %copy-done.9 = f32[1024]{0:T(1024)S(1)} copy-done((f32[1024]{0:T(1024)S(1)}, f32[1024]{0:T(1024)}, u32[]{:S(2)}) %copy-start.9) | copy-done | bytes 4120
  11.4 0.0 copy-start.10
  11.4 0.7 %copy-done.10 = f32[1024]{0:T(1024)S(1)} copy-done((f32[1024]{0:T(1024)S(1)}, f32[1024]{0:T(1024)}, u32[]{:S(2)}) %copy-start.10) | copy-done | bytes 4120
  12.1 0.0 copy-start.11
  12.1 0.7 %copy-done.11 = f32[1024]{0:T(1024)S(1)} copy-done((f32[1024]{0:T(1024)S(1)}, f32[1024]{0:T(1024)}, u32[]{:S(2)}) %copy-start.11) | copy-done | bytes 4120
  12.8 39.2 %shard_map.118 = bf16[1024,128]{1,0:T(8,128)(2,1)S(1)} custom-call(bf16[1024,128]{1,0:T(8,128)(2,1)S(1)} %copy-done.1, bf16[1024,128]{1,0:T(8,128)(2,1)S(1)} %copy-done.2, bf16[1024,128]{1,0:T(8,128)(2,1)S(1)} %copy-done.3, bf16[1024,128]{1,0:T(8,128)(2,1)S(1)} %copy-done.4, bf16[1024,128]{1,0:T(8,128)(2,1)S(1)} %copy-done.5, ...), custom_call_target="tpu_custom_call" | custom-call | tf_op jit(solution)/shard_map/pallas_call | solution.py:426
  52.0 0.7 %copy.14 = bf16[1024,128]{1,0:T(8,128)(2,1)} copy(bf16[1024,128]{1,0:T(8,128)(2,1)S(1)} %shard_map.118) | data formatting | bytes 524288
Async XLA Ops:
  0.0 3.4 %copy-start = (bf16[4096,1024]{1,0:T(8,128)(2,1)S(1)}, bf16[4096,1024]{1,0:T(8,128)(2,1)}, u32[]{:S(2)}) copy-start(bf16[4096,1024]{1,0:T(8,128)(2,1)} %wt_hbm.1) | copy-start | bytes 25165828
  3.4 0.9 %copy-start.1 = (bf16[1024,128]{1,0:T(8,128)(2,1)S(1)}, bf16[1024,128]{1,0:T(8,128)(2,1)}, u32[]{:S(2)}) copy-start(bf16[1024,128]{1,0:T(8,128)(2,1)} %skip_ref.1) | copy-start | bytes 786436
  4.3 0.9 %copy-start.2 = (bf16[1024,128]{1,0:T(8,128)(2,1)S(1)}, bf16[1024,128]{1,0:T(8,128)(2,1)}, u32[]{:S(2)}) copy-start(bf16[1024,128]{1,0:T(8,128)(2,1)} %r_ref.1) | copy-start | bytes 786436
  5.3 0.9 %copy-start.3 = (bf16[1024,128]{1,0:T(8,128)(2,1)S(1)}, bf16[1024,128]{1,0:T(8,128)(2,1)}, u32[]{:S(2)}) copy-start(bf16[1024,128]{1,0:T(8,128)(2,1)} %k_ref.1) | copy-start | bytes 786436
  6.2 0.9 %copy-start.4 = (bf16[1024,128]{1,0:T(8,128)(2,1)S(1)}, bf16[1024,128]{1,0:T(8,128)(2,1)}, u32[]{:S(2)}) copy-start(bf16[1024,128]{1,0:T(8,128)(2,1)} %v_ref.1) | copy-start | bytes 786436
  7.2 0.9 %copy-start.5 = (bf16[1024,128]{1,0:T(8,128)(2,1)S(1)}, bf16[1024,128]{1,0:T(8,128)(2,1)}, u32[]{:S(2)}) copy-start(bf16[1024,128]{1,0:T(8,128)(2,1)} %g_ref.1) | copy-start | bytes 786436
  8.1 0.9 %copy-start.6 = (bf16[1024,128]{1,0:T(8,128)(2,1)S(1)}, bf16[1024,128]{1,0:T(8,128)(2,1)}, u32[]{:S(2)}) copy-start(bf16[1024,128]{1,0:T(8,128)(2,1)} %w_ref.1) | copy-start | bytes 786436
  9.1 0.9 %copy-start.7 = (bf16[1024,128]{1,0:T(8,128)(2,1)S(1)}, bf16[1024,128]{1,0:T(8,128)(2,1)}, u32[]{:S(2)}) copy-start(bf16[1024,128]{1,0:T(8,128)(2,1)} %a_ref.1) | copy-start | bytes 786436
  10.0 0.7 %copy-start.8 = (f32[1024]{0:T(1024)S(1)}, f32[1024]{0:T(1024)}, u32[]{:S(2)}) copy-start(f32[1024]{0:T(1024)} %param.19) | copy-start | bytes 12292
  10.7 0.7 %copy-start.9 = (f32[1024]{0:T(1024)S(1)}, f32[1024]{0:T(1024)}, u32[]{:S(2)}) copy-start(f32[1024]{0:T(1024)} %param.20) | copy-start | bytes 12292
  11.4 0.7 %copy-start.10 = (f32[1024]{0:T(1024)S(1)}, f32[1024]{0:T(1024)}, u32[]{:S(2)}) copy-start(f32[1024]{0:T(1024)} %param.21) | copy-start | bytes 12292
  12.1 0.7 %copy-start.11 = (f32[1024]{0:T(1024)S(1)}, f32[1024]{0:T(1024)}, u32[]{:S(2)}) copy-start(f32[1024]{0:T(1024)} %param.22) | copy-start | bytes 12292
where the time goes:
time: 53.2 us; the launch traced here: 52.7 us
  Pallas kernels  39.2 us (74%)
  local copies, waits for them, and re-layouts  13.5 us (25%)
    pallas_call x1, Pallas kernels, on_device(): pl.pallas_call(kernel, out_shape=jax.ShapeDtypeStruct((ROWS, TOK), BF16),...  39.2 us
    unnamed x25, local copies, waits for them, and re-layouts  13.5 us

commit v1 on v0

--- a/solution.py
+++ b/solution.py
@@ -40,13 +40,14 @@
 
 
 def kernel(
-    skip_ref, r_ref, k_ref, v_ref, g_ref, w_ref, a_ref, ef_ref, rc_ref, gm_ref, gb_ref, wt_hbm,
+    skip_hbm, r_hbm, k_hbm, v_hbm, g_hbm, w_hbm, a_hbm, ef_hbm, rc_hbm, gm_hbm, gb_hbm, wt_hbm,
     out_ref,
+    skip_ref, r_ref, k_ref, v_ref, g_ref, w_ref, a_ref, ef_ref, rc_ref, gm_ref, gb_ref,
     par, comb, read, local, inbox, prefix, outbox, entering, mixed, weights,
     send_a, got_a, held_b, send_b, got_b, total,
     masks, pull_t, key_t, ends_t, ahead_s, pair_s, pread_s, kread_s, inv_s, inv, part_s, seen_s,
     recv_s, decay_s, solved_s, rest,
-    wt_sem, comb_send, comb_recv, state_send, state_recv, rs_send, rs_recv,
+    in_sem, wt_sem, comb_send, comb_recv, state_send, state_recv, rs_send, rs_recv,
 ):
     head = lax.axis_index("head")
     me = lax.axis_index("seq")
@@ -59,6 +60,14 @@
         x = 2 * (place % 2) + (y + odd) % 2
         return y * 8 + x * 2 + (odd + core) % 2
 
+    first = ((ef_hbm, ef_ref), (w_hbm, w_ref), (k_hbm, k_ref), (a_hbm, a_ref), (r_hbm, r_ref), (v_hbm, v_ref))
+    second = ((rc_hbm, rc_ref), (gm_hbm, gm_ref), (gb_hbm, gb_ref), (g_hbm, g_ref), (skip_hbm, skip_ref))
+    first = [pltpu.make_async_copy(*pair, in_sem.at[n]) for n, pair in enumerate(first)]
+    second = [pltpu.make_async_copy(*pair, in_sem.at[6 + n]) for n, pair in enumerate(second)]
+    wt_copy = pltpu.make_async_copy(wt_hbm, weights, wt_sem)
+    for copy in first + second + [wt_copy]:
+        copy.start()
+
     barrier = pltpu.get_barrier_semaphore()
 
     def greet(d, carry):
@@ -76,13 +85,13 @@
         return carry
 
     lax.fori_loop(1, 4, greet_head, 0)
-    wt_copy = pltpu.make_async_copy(wt_hbm, weights, wt_sem)
-    wt_copy.start()
 
     def spread(p, ref):
         for j in range(8):
             par[p, j * 128 : (j + 1) * 128, :] = jnp.broadcast_to(ref[j : j + 1, :], (128, 128)).T
 
+    for copy in first:
+        copy.wait()
     spread(0, ef_ref)
 
     row = lax.broadcasted_iota(jnp.int32, (TOK, TOK), 0)
@@ -229,6 +238,8 @@
         if base == 0:
             pl.semaphore_wait(barrier, SLABS - 1 + 3)
         lax.fori_loop(base, base + BATCH, send_comb, 0)
+    for copy in second:
+        copy.wait()
     spread(1, rc_ref)
     spread(2, gm_ref)
     spread(3, gb_ref)
@@ -303,11 +314,14 @@
                 done = prefix[g * GROUP + i - 1]
                 pack(g * GROUP + i, dot(starts[g], done[CH:]) + done[:CH])
 
-        def give(d, carry):
-            state_copy(lax.rem(me + d, SLABS)).start()
-            return carry
-
-        lax.fori_loop(1, SLABS, give, 0)
+        for _, dy, dx, dz in sorted(
+            (-min(dy, 4 - dy) - min(dx, 4 - dx) - dz, dy, dx, dz)
+            for dy in range(4)
+            for dx in range(4)
+            for dz in range(2)
+            if dy + dx + dz
+        ):
+            state_copy((my_y + dy) % 4 * 8 + (my_x + dx) % 4 * 2 + (me + dz) % 2).start()
         entering[my_head] = outbox[me]
 
     def arrived(h):
@@ -426,9 +440,11 @@
     return pl.pallas_call(
         kernel,
         out_shape=jax.ShapeDtypeStruct((ROWS, TOK), BF16),
-        in_specs=[vmem] * 11 + [pl.BlockSpec(memory_space=pl.ANY)],
+        in_specs=[pl.BlockSpec(memory_space=pltpu.HBM)] * 12,
         out_specs=vmem,
-        scratch_shapes=[
+        scratch_shapes=[pltpu.VMEM((ROWS, TOK), BF16)] * 7
+        + [pltpu.VMEM((8, 128), F32)] * 4
+        + [
             pltpu.VMEM((4, ROWS, TOK), F32),
             pltpu.VMEM((HEADS, CH + EXTRA, 2 * CH), BF16),
             pltpu.VMEM((HEADS, 2 * CH, TOK), BF16),
@@ -461,6 +477,7 @@
             pltpu.VMEM((BATCH, CH, TOK), F32),
             pltpu.VMEM((HEADS, TOK, 2 * TOK), BF16),
             pltpu.VMEM((HEADS, CH, TOK), F32),
+            dma((11,)),
             dma(()),
             dma((HEADS,)),
             dma((SLABS,)),
@@ -472,7 +489,9 @@
         compiler_params=pltpu.CompilerParams(
             collective_id=0, has_side_effects=True, vmem_limit_bytes=40 * 1024 * 1024
         ),
-    )(skip, r, k, v, g, w, a, *(p.reshape(8, 128) for p in (ef, rc, gm, gb)), wt)
+    )(*(
+        pltpu.with_memory_space_constraint(x, pltpu.HBM) for x in (skip, r, k, v, g, w, a, *(p.reshape(8, 128) for p in (ef, rc, gm, gb)), wt)
+    ))
 
 
 def solution(mesh):

time: 53.2 us -> 40.4 us (0.76)
  local copies, waits for them, and re-layouts: 13.5 us -> 0.71 us
    unnamed x25 -> x1, local copies, waits for them, and re-layouts: 13.5 us -> 0.71 us
where the time goes in v1:
time: 40.4 us; the launch traced here: 40.3 us
  Pallas kernels  39.5 us (98%)
  local copies, waits for them, and re-layouts  0.71 us (2%)
    pallas_call x1, Pallas kernels, on_device(): pl.pallas_call(kernel, out_shape=jax.ShapeDtypeStruct((ROWS, TOK), BF16),...  39.5 us

profile of v1, /device:TPU:1, one launch (start us, length us, event | category | flops | bytes accessed | tf_op | source)
XLA Modules:
  0.0 40.3 jit_solution(5907100343295341792)
XLA Ops:
  0.0 39.5 %shard_map.118 = bf16[1024,128]{1,0:T(8,128)(2,1)S(1)} custom-call(bf16[1024,128]{1,0:T(8,128)(2,1)} %skip_hbm.1, bf16[1024,128]{1,0:T(8,128)(2,1)} %r_hbm.1, bf16[1024,128]{1,0:T(8,128)(2,1)} %k_hbm.1, bf16[1024,128]{1,0:T(8,128)(2,1)} %v_hbm.1, bf16[1024,128]{1,0:T(8,128)(2,1)} %g_hbm.1, bf16[1024,128]{1,0:T(8,128)(2,1)} %w_hbm.1, ...), custom_call_target="tpu_custom_call" | custom-call | tf_op jit(solution)/shard_map/pallas_call | solution.py:440
  39.6 0.7 %copy.14 = bf16[1024,128]{1,0:T(8,128)(2,1)} copy(bf16[1024,128]{1,0:T(8,128)(2,1)S(1)} %shard_map.118) | data formatting | bytes 524288

commit v2 on v1

--- a/solution.py
+++ b/solution.py
@@ -20,12 +20,6 @@
 BF16 = jnp.bfloat16
 
 
-def dot(left, right, dims=((1,), (0,)), precision=lax.Precision.HIGH):
-    return lax.dot_general(
-        left, right, (dims, ((), ())), precision=precision, preferred_element_type=F32
-    )
-
-
 def halves(x):
     high = x.astype(BF16)
     return high, (x - high.astype(F32)).astype(BF16)
@@ -46,13 +40,13 @@
     par, comb, read, local, inbox, prefix, outbox, entering, mixed, weights,
     send_a, got_a, held_b, send_b, got_b, total,
     masks, pull_t, key_t, ends_t, ahead_s, pair_s, pread_s, kread_s, inv_s, inv, part_s, seen_s,
-    recv_s, decay_s, solved_s, rest,
+    recv_s, decay_s, solved_s, rest, pair, both,
     in_sem, wt_sem, comb_send, comb_recv, state_send, state_recv, rs_send, rs_recv,
 ):
     head = lax.axis_index("head")
     me = lax.axis_index("seq")
     core = lax.rem(head, 2)
-    pair = head // 2
+    chip = head // 2
 
     def owner_of(h):
         odd, place = h // 8, h % 8
@@ -97,8 +91,9 @@
     row = lax.broadcasted_iota(jnp.int32, (TOK, TOK), 0)
     col = lax.broadcasted_iota(jnp.int32, (TOK, TOK), 1)
     upto = jnp.where(row <= col, 1.0, 0.0).astype(BF16)
-    for level in range(7):
-        masks[level] = jnp.where(((row ^ col) >> level) == 1, 1.0, 0.0).astype(BF16)
+    apart = row ^ col
+    near = (apart >= 2) & (apart < 16)
+    masks[...] = jnp.where(apart >= 16, 1.0, 0.0).astype(BF16)
     zero = jnp.zeros((TOK, TOK), BF16)
     diag = lax.broadcasted_iota(jnp.int32, (CH, TOK), 0) == lax.broadcasted_iota(
         jnp.int32, (CH, TOK), 1
@@ -119,6 +114,11 @@
 
     def turned(x):
         return jnp.concatenate(halves(x), axis=0).T
+
+    def two_diag(one, other):
+        return jnp.concatenate(
+            [jnp.concatenate([one, zero], axis=1), jnp.concatenate([zero, other], axis=1)], axis=0
+        )
 
     def group_local(base):
         for i in range(BATCH):
@@ -155,10 +155,12 @@
             pull = pull_t[i]
             from_pull = mm(jnp.concatenate([pull, pull], axis=1), ahead)
             pair_mix = jnp.where(row < col, from_pull[:, :TOK], 0.0)
+            pair[i] = pair_mix
             pair_s[i] = beside(pair_mix)
-            start = jnp.where(row == col, 1.0, pair_mix * masks[0].astype(F32))
+            start = jnp.where(apart == 1, pair_mix, 0.0)
             inv[i] = start
-            inv_s[i] = beside(start)
+            both[i, TOK:, :TOK] = start.astype(BF16)
+            both[i, :TOK, :TOK] = jnp.where(near, pair_mix, 0.0).astype(BF16)
             pread_s[base + i] = from_pull[:, TOK:]
             key = key_t[i]
             from_key = mm(jnp.concatenate([key, key], axis=1), ahead)
@@ -167,18 +169,54 @@
         for i in range(BATCH):
             rows = slice((base + i) * CH, (base + i + 1) * CH)
             seen_s[i, :CH, :] = fold(mm(v_ref[rows, :], part_s[i]))
-        for level in range(1, 7):
-            mask = masks[level]
+        for i in range(0, BATCH, 2):
+            res = mm(
+                jnp.concatenate([both[i, :TOK, :TOK], both[i + 1, :TOK, :TOK]], axis=1),
+                two_diag(both[i, TOK:, :TOK], both[i + 1, TOK:, :TOK]),
+            )
+            for n in range(2):
+                e = jnp.where(near, pair[i + n], 0.0) + res[:, n * TOK : (n + 1) * TOK]
+                both[i + n, :TOK, :TOK] = e.astype(BF16)
+                inv[i + n] = inv[i + n] + e
+        for _ in range(2):
+            for i in range(0, BATCH, 2):
+                res = mm(
+                    jnp.concatenate([both[i, :, :TOK], both[i + 1, :, :TOK]], axis=1),
+                    two_diag(both[i, :TOK, :TOK], both[i + 1, :TOK, :TOK]),
+                )
+                for n in range(2):
+                    e = res[:TOK, n * TOK : (n + 1) * TOK]
+                    m = inv[i + n] + res[TOK:, n * TOK : (n + 1) * TOK]
+                    both[i + n, :TOK, :TOK] = e.astype(BF16)
+                    both[i + n, TOK:, :TOK] = m.astype(BF16)
+                    inv[i + n] = m + e
+        for i in range(0, BATCH, 2):
+            res = mm(
+                jnp.concatenate([both[i, TOK:, :TOK], both[i + 1, TOK:, :TOK]], axis=1),
+                two_diag(both[i, :TOK, :TOK], both[i + 1, :TOK, :TOK]),
+            )
+            for n in range(2):
+                whole = jnp.where(row == col, 1.0, inv[i + n] + res[:, n * TOK : (n + 1) * TOK])
+                inv_s[i + n] = beside(whole)
+        for i in range(BATCH):
+            left = jnp.concatenate(
+                [pair_s[i] * jnp.concatenate([masks[...], masks[...]], axis=1), beside(seen_s[i])],
+                axis=0,
+            )
+            res = fold(mm(left, wide(inv_s[i])))
+            both[i] = beside(res)
+            inv[i] = res[TOK:]
+        for _ in range(2):
             for i in range(BATCH):
-                off = pair_s[i] * jnp.concatenate([mask, mask], axis=1)
-                part_s[i] = beside(fold(mm(inv_s[i], wide(off))))
-            for i in range(BATCH):
-                new = inv[i] + fold(mm(part_s[i], wide(inv_s[i])))
-                if level < 6:
-                    inv[i] = new
-                inv_s[i] = beside(new)
-        for i in range(BATCH):
-            solved_s[base + i] = beside(fold(mm(beside(seen_s[i]), wide(inv_s[i]))))
+                res = fold(mm(both[i], wide(both[i, :TOK, :])))
+                g = inv[i] + res[TOK:]
+                both[i, :TOK, :] = beside(res[:TOK])
+                both[i, TOK:, :] = beside(g)
+                inv[i] = g
+        for i in range(BATCH):
+            solved_s[base + i] = beside(
+                inv[i] + fold(mm(both[i, TOK:, :], wide(both[i, :TOK, :])))
+            )
         for i in range(BATCH):
             h = base + i
             rows = slice(h * CH, (h + 1) * CH)
@@ -276,43 +314,58 @@
         lax.fori_loop(1, SLABS, arrive, 0)
 
         def pack(i, value):
-            value = value.astype(BF16)
-            outbox[i] = jnp.concatenate([value[: CH // 2], value[CH // 2 :]], axis=1)
+            half = CH // 2
+            outbox[i] = jnp.where(left_half[:half], value[:half], value[half:]).astype(BF16)
 
         def item_of(i):
-            item = inbox[i]
-            trans = item[:CH, :CH]
-            state = pltpu.roll(item[:CH].astype(F32), CH, 1)[:, :CH]
-            return trans, item[CH : CH + 1, :CH].astype(F32), state
-
+            item = inbox[i].astype(F32)
+            swapped = pltpu.roll(item, CH, 1)
+            trans = jnp.where(left_half, item[:CH], swapped[:CH])
+            state = jnp.where(left_half, swapped[:CH], item[:CH])
+            missed = jnp.where(left_half[:1], item[CH : CH + 1], swapped[CH : CH + 1])
+            return trans, missed, state
+
+        def left_of(x):
+            return jnp.where(wide_half[: x.shape[0]], x, x - x.astype(BF16).astype(F32)).astype(BF16)
+
+        def right_of(x):
+            high, low = halves(x)
+            none = jnp.zeros((CH, TOK), BF16)
+            return jnp.concatenate(
+                [jnp.concatenate([high, low], axis=1), jnp.concatenate([high, none], axis=1)],
+                axis=0,
+            )
+
+        wide_half = lax.broadcasted_iota(jnp.int32, (TOK, TOK), 1) < CH
         groups = SLABS // GROUP
         for g in range(groups):
             trans, missed, state = item_of(g * GROUP)
-            whole = trans.astype(F32) + jnp.where(diag[:, :CH], missed, 0.0)
-            prefix[g * GROUP] = jnp.concatenate([state, whole], axis=0)
+            prefix[g * GROUP, :CH, :] = state
+            prefix[g * GROUP, CH:, :] = trans + jnp.where((row % CH == col % CH)[:CH], missed, 0.0)
 
         def step(i, carry):
             for g in range(groups):
                 trans, missed, state = item_of(g * GROUP + i)
+                trans = trans.astype(BF16)
                 old = prefix[g * GROUP + i - 1]
-                high, low = halves(old)
-                moved = mm(high, trans) + mm(low, trans) + old * missed
+                moved = mm(left_of(old), jnp.concatenate([trans, trans], axis=0)) + old * missed
                 prefix[g * GROUP + i, :CH, :] = moved[:CH] + state
                 prefix[g * GROUP + i, CH:, :] = moved[CH:]
             return carry
 
         lax.fori_loop(1, GROUP, step, 0)
-        start = jnp.zeros((CH, CH), F32)
+        start = jnp.zeros((CH, TOK), F32)
         starts = [start]
         for g in range(groups - 1):
             done = prefix[g * GROUP + GROUP - 1]
-            start = dot(start, done[CH:]) + done[:CH]
+            start = done[:CH] if g == 0 else fold(mm(left_of(start), right_of(done[CH:]))) + done[:CH]
             starts.append(start)
         for g in range(groups):
             pack(g * GROUP, starts[g])
             for i in range(1, GROUP):
                 done = prefix[g * GROUP + i - 1]
-                pack(g * GROUP + i, dot(starts[g], done[CH:]) + done[:CH])
+                moved = fold(mm(left_of(starts[g]), right_of(done[CH:]))) if g else 0.0
+                pack(g * GROUP + i, moved + done[:CH])
 
         for _, dy, dx, dz in sorted(
             (-min(dy, 4 - dy) - min(dx, 4 - dx) - dz, dy, dx, dz)
@@ -360,12 +413,12 @@
             mixed[rows, :] = ((normed + rest[base + i]) * g_ref[rows, :].astype(F32)).astype(BF16)
 
     wt_copy.wait()
-    partner = pair * 2 + 1 - core
-    across = (1 - pair) * 2 + core
+    partner = chip * 2 + 1 - core
+    across = (1 - chip) * 2 + core
 
     def piece(dest, c):
         rows = pl.ds(pl.multiple_of(dest * ROWS + c * CHUNK, CHUNK), CHUNK)
-        return dot(weights[rows, :], mixed[...], precision=None)
+        return mm(weights[rows, :], mixed[...])
 
     pieces = ROWS // CHUNK
 
@@ -390,7 +443,7 @@
         )
 
     for c in range(pieces):
-        send_a[c] = piece((1 - pair) * 2 + 1 - core, c)
+        send_a[c] = piece((1 - chip) * 2 + 1 - core, c)
         near_copy(c).start()
     for c in range(pieces):
         held_b[c] = piece(across, c)
@@ -450,7 +503,7 @@
             pltpu.VMEM((HEADS, 2 * CH, TOK), BF16),
             pltpu.VMEM((HEADS, CH, TOK), F32),
             pltpu.VMEM((SLABS, CH + EXTRA, 2 * CH), BF16),
-            pltpu.VMEM((SLABS, 2 * CH, CH), F32),
+            pltpu.VMEM((SLABS, TOK, TOK), F32),
             pltpu.VMEM((SLABS, CH // 2, 2 * CH), BF16),
             pltpu.VMEM((HEADS, CH // 2, 2 * CH), BF16),
             pltpu.VMEM((ROWS, TOK), BF16),
@@ -461,7 +514,7 @@
             pltpu.VMEM((pieces, CHUNK, TOK), BF16),
             pltpu.VMEM((pieces, CHUNK, TOK), BF16),
             pltpu.VMEM((ROWS, TOK), F32),
-            pltpu.VMEM((7, TOK, TOK), BF16),
+            pltpu.VMEM((TOK, TOK), BF16),
             pltpu.VMEM((BATCH, TOK, TOK), BF16),
             pltpu.VMEM((BATCH, TOK, TOK), BF16),
             pltpu.VMEM((BATCH, TOK, 2 * TOK), BF16),
@@ -477,6 +530,8 @@
             pltpu.VMEM((BATCH, CH, TOK), F32),
             pltpu.VMEM((HEADS, TOK, 2 * TOK), BF16),
             pltpu.VMEM((HEADS, CH, TOK), F32),
+            pltpu.VMEM((BATCH, TOK, TOK), F32),
+            pltpu.VMEM((BATCH, 2 * TOK, 2 * TOK), BF16),
             dma((11,)),
             dma(()),
             dma((HEADS,)),

time: 40.4 us -> 40 us (0.990)
  no operation moved by 1% of the time
where the time goes in v2:
time: 40 us; the launch traced here: 39.9 us
  Pallas kernels  39.2 us (98%)
  local copies, waits for them, and re-layouts  0.71 us (2%)
    pallas_call x1, Pallas kernels, on_device(): pl.pallas_call(kernel, out_shape=jax.ShapeDtypeStruct((ROWS, TOK), BF16),...  39.2 us

profile of v2, /device:TPU:1, one launch (start us, length us, event | category | flops | bytes accessed | tf_op | source)
XLA Modules:
  0.0 39.9 jit_solution(3106467409229688837)
XLA Ops:
  0.0 39.2 %shard_map.118 = bf16[1024,128]{1,0:T(8,128)(2,1)S(1)} custom-call(bf16[1024,128]{1,0:T(8,128)(2,1)} %skip_hbm.1, bf16[1024,128]{1,0:T(8,128)(2,1)} %r_hbm.1, bf16[1024,128]{1,0:T(8,128)(2,1)} %k_hbm.1, bf16[1024,128]{1,0:T(8,128)(2,1)} %v_hbm.1, bf16[1024,128]{1,0:T(8,128)(2,1)} %g_hbm.1, bf16[1024,128]{1,0:T(8,128)(2,1)} %w_hbm.1, ...), custom_call_target="tpu_custom_call" | custom-call | tf_op jit(solution)/shard_map/pallas_call | solution.py:493
  39.2 0.7 %copy.14 = bf16[1024,128]{1,0:T(8,128)(2,1)} copy(bf16[1024,128]{1,0:T(8,128)(2,1)S(1)} %shard_map.118) | data formatting | bytes 524288

commit v3 on v2

--- a/solution.py
+++ b/solution.py
@@ -15,7 +15,7 @@
 EXTRA = 16
 GROUP = 8
 BATCH = 8
-CHUNK = 256
+CHUNK = 128
 F32 = jnp.float32
 BF16 = jnp.bfloat16
 
@@ -39,8 +39,8 @@
     skip_ref, r_ref, k_ref, v_ref, g_ref, w_ref, a_ref, ef_ref, rc_ref, gm_ref, gb_ref,
     par, comb, read, local, inbox, prefix, outbox, entering, mixed, weights,
     send_a, got_a, held_b, send_b, got_b, total,
-    masks, pull_t, key_t, ends_t, ahead_s, pair_s, pread_s, kread_s, inv_s, inv, part_s, seen_s,
-    recv_s, decay_s, solved_s, rest, pair, both,
+    pull_t, key_t, ends_t, ahead_s, pair_s, inv_s, inv, part_s, seen_s,
+    recv_s, decay_s, solved_s, rest, both,
     in_sem, wt_sem, comb_send, comb_recv, state_send, state_recv, rs_send, rs_recv,
 ):
     head = lax.axis_index("head")
@@ -59,7 +59,7 @@
     first = [pltpu.make_async_copy(*pair, in_sem.at[n]) for n, pair in enumerate(first)]
     second = [pltpu.make_async_copy(*pair, in_sem.at[6 + n]) for n, pair in enumerate(second)]
     wt_copy = pltpu.make_async_copy(wt_hbm, weights, wt_sem)
-    for copy in first + second + [wt_copy]:
+    for copy in first:
         copy.start()
 
     barrier = pltpu.get_barrier_semaphore()
@@ -86,6 +86,8 @@
 
     for copy in first:
         copy.wait()
+    for copy in second + [wt_copy]:
+        copy.start()
     spread(0, ef_ref)
 
     row = lax.broadcasted_iota(jnp.int32, (TOK, TOK), 0)
@@ -93,7 +95,6 @@
     upto = jnp.where(row <= col, 1.0, 0.0).astype(BF16)
     apart = row ^ col
     near = (apart >= 2) & (apart < 16)
-    masks[...] = jnp.where(apart >= 16, 1.0, 0.0).astype(BF16)
     zero = jnp.zeros((TOK, TOK), BF16)
     diag = lax.broadcasted_iota(jnp.int32, (CH, TOK), 0) == lax.broadcasted_iota(
         jnp.int32, (CH, TOK), 1
@@ -135,37 +136,28 @@
             at_mid = jnp.exp(mid)
             to_end = back * jnp.exp(end - mid)
             removal_fwd = -removal * jnp.exp(running - w16.astype(F32) - mid)
-            recept_fwd = r_ref[rows, :].astype(F32) * jnp.exp(running - mid)
-            pull_t[i] = turned(pulled * back)
-            key_t[i] = turned(kf * back)
+            pull_t[base + i] = turned(pulled * back)
+            key_t[base + i] = turned(kf * back)
             ends_t[i, :, :TOK] = turned(pulled * to_end)
             ends_t[i, :, TOK:] = turned(kf * to_end)
             rem_hi, rem_lo = halves(removal_fwd)
-            rec_hi, rec_lo = halves(recept_fwd)
-            ahead_s[i, :CH, :TOK] = rem_hi
-            ahead_s[i, CH:, :TOK] = rem_lo
-            ahead_s[i, :CH, TOK:] = rec_hi
-            ahead_s[i, CH:, TOK:] = rec_lo
+            ahead_s[i, :CH, :] = rem_hi
+            ahead_s[i, CH:, :] = rem_lo
             seen_s[i, CH:, :] = removal_fwd * at_mid
-            recv_s[base + i] = recept_fwd * at_mid
             decay_s[i] = jnp.where(diag, jnp.exp(end), 0.0)
         for i in range(BATCH):
             ahead = ahead_s[i]
             ahead = jnp.concatenate([ahead[:CH], ahead[:CH], ahead[CH:], ahead[CH:]], axis=0)
-            pull = pull_t[i]
+            pull = pull_t[base + i]
             from_pull = mm(jnp.concatenate([pull, pull], axis=1), ahead)
-            pair_mix = jnp.where(row < col, from_pull[:, :TOK], 0.0)
-            pair[i] = pair_mix
-            pair_s[i] = beside(pair_mix)
-            start = jnp.where(apart == 1, pair_mix, 0.0)
-            inv[i] = start
-            both[i, TOK:, :TOK] = start.astype(BF16)
+            pair_mix = jnp.where(row < col, from_pull, 0.0)
+            pair_s[i] = beside(jnp.where(apart >= 16, pair_mix, 0.0))
+            inv[i] = jnp.where(apart < 16, pair_mix, 0.0)
+            both[i, TOK:, :TOK] = jnp.where(apart == 1, pair_mix, 0.0).astype(BF16)
             both[i, :TOK, :TOK] = jnp.where(near, pair_mix, 0.0).astype(BF16)
-            pread_s[base + i] = from_pull[:, TOK:]
-            key = key_t[i]
+            key = key_t[base + i]
             from_key = mm(jnp.concatenate([key, key], axis=1), ahead)
-            kread_s[base + i] = from_key[:, TOK:]
-            part_s[i] = beside(jnp.where(row < col, from_key[:, :TOK], 0.0))
+            part_s[i] = beside(jnp.where(row < col, from_key, 0.0))
         for i in range(BATCH):
             rows = slice((base + i) * CH, (base + i + 1) * CH)
             seen_s[i, :CH, :] = fold(mm(v_ref[rows, :], part_s[i]))
@@ -175,9 +167,9 @@
                 two_diag(both[i, TOK:, :TOK], both[i + 1, TOK:, :TOK]),
             )
             for n in range(2):
-                e = jnp.where(near, pair[i + n], 0.0) + res[:, n * TOK : (n + 1) * TOK]
-                both[i + n, :TOK, :TOK] = e.astype(BF16)
-                inv[i + n] = inv[i + n] + e
+                more = res[:, n * TOK : (n + 1) * TOK]
+                both[i + n, :TOK, :TOK] = (both[i + n, :TOK, :TOK].astype(F32) + more).astype(BF16)
+                inv[i + n] = inv[i + n] + more
         for _ in range(2):
             for i in range(0, BATCH, 2):
                 res = mm(
@@ -199,10 +191,7 @@
                 whole = jnp.where(row == col, 1.0, inv[i + n] + res[:, n * TOK : (n + 1) * TOK])
                 inv_s[i + n] = beside(whole)
         for i in range(BATCH):
-            left = jnp.concatenate(
-                [pair_s[i] * jnp.concatenate([masks[...], masks[...]], axis=1), beside(seen_s[i])],
-                axis=0,
-            )
+            left = jnp.concatenate([pair_s[i], beside(seen_s[i])], axis=0)
             res = fold(mm(left, wide(inv_s[i])))
             both[i] = beside(res)
             inv[i] = res[TOK:]
@@ -237,11 +226,23 @@
         for i in range(BATCH):
             h = base + i
             rows = slice(h * CH, (h + 1) * CH)
-            pread = beside(jnp.where(row <= col, pread_s[h], 0.0))
-            kread = beside(jnp.where(row <= col, kread_s[h], 0.0))
-            out = fold(mm(solved_s[h], wide(pread)))
-            local[h] = out[:CH] + fold(mm(v_ref[rows, :], kread))
-            read[h] = jnp.concatenate(halves(out[CH:] + recv_s[h]), axis=0)
+            running = mm(w_ref[rows, :], upto)
+            mid = running[:, 63:64]
+            recept_fwd = r_ref[rows, :].astype(F32) * jnp.exp(running - mid)
+            recv_s[i] = recept_fwd * jnp.exp(mid)
+            high, low = halves(recept_fwd)
+            ahead = jnp.concatenate([high, high, low, low], axis=0)
+            pull, key = pull_t[h], key_t[h]
+            pread = mm(jnp.concatenate([pull, pull], axis=1), ahead)
+            kread = mm(jnp.concatenate([key, key], axis=1), ahead)
+            pair_s[i] = beside(jnp.where(row <= col, pread, 0.0))
+            part_s[i] = beside(jnp.where(row <= col, kread, 0.0))
+        for i in range(BATCH):
+            h = base + i
+            rows = slice(h * CH, (h + 1) * CH)
+            out = fold(mm(solved_s[h], wide(pair_s[i])))
+            local[h] = out[:CH] + fold(mm(v_ref[rows, :], part_s[i]))
+            read[h] = jnp.concatenate(halves(out[CH:] + recv_s[i]), axis=0)
             kf = k_ref[rows, :].astype(F32)
             vf = v_ref[rows, :].astype(F32)
             rf = r_ref[rows, :].astype(F32)
@@ -458,15 +459,8 @@
         total[rows, :] = piece(head, c) + skip_ref[rows, :].astype(F32)
         near_copy(pieces + c).wait_recv()
         total[rows, :] = total[rows, :] + got_a[pieces + c]
-    for c in range(pieces):
-        rows = slice(c * CHUNK, (c + 1) * CHUNK)
-        far_copy(c).wait_recv()
-        out_ref[rows, :] = (total[rows, :] + got_b[c].astype(F32)).astype(BF16)
-
     for c in range(2 * pieces):
         near_copy(c).wait_send()
-    for c in range(pieces):
-        far_copy(c).wait_send()
 
     def sent_comb(h, carry):
         @pl.when(owner_of(h) != me)
@@ -484,6 +478,13 @@
             return carry
 
         lax.fori_loop(1, SLABS, sent_state, 0)
+
+    for c in range(pieces):
+        rows = slice(c * CHUNK, (c + 1) * CHUNK)
+        far_copy(c).wait_recv()
+        out_ref[rows, :] = (total[rows, :] + got_b[c].astype(F32)).astype(BF16)
+    for c in range(pieces):
+        far_copy(c).wait_send()
 
 
 def on_device(skip, r, k, v, g, w, a, ef, rc, gm, gb, wt):
@@ -514,23 +515,19 @@
             pltpu.VMEM((pieces, CHUNK, TOK), BF16),
             pltpu.VMEM((pieces, CHUNK, TOK), BF16),
             pltpu.VMEM((ROWS, TOK), F32),
-            pltpu.VMEM((TOK, TOK), BF16),
-            pltpu.VMEM((BATCH, TOK, TOK), BF16),
+            pltpu.VMEM((HEADS, TOK, TOK), BF16),
+            pltpu.VMEM((HEADS, TOK, TOK), BF16),
+            pltpu.VMEM((BATCH, TOK, 2 * TOK), BF16),
             pltpu.VMEM((BATCH, TOK, TOK), BF16),
             pltpu.VMEM((BATCH, TOK, 2 * TOK), BF16),
-            pltpu.VMEM((BATCH, TOK, 2 * TOK), BF16),
-            pltpu.VMEM((BATCH, TOK, 2 * TOK), BF16),
-            pltpu.VMEM((HEADS, TOK, TOK), F32),
-            pltpu.VMEM((HEADS, TOK, TOK), F32),
             pltpu.VMEM((BATCH, TOK, 2 * TOK), BF16),
             pltpu.VMEM((BATCH, TOK, TOK), F32),
             pltpu.VMEM((BATCH, TOK, 2 * TOK), BF16),
             pltpu.VMEM((BATCH, TOK, TOK), F32),
-            pltpu.VMEM((HEADS, CH, TOK), F32),
+            pltpu.VMEM((BATCH, CH, TOK), F32),
             pltpu.VMEM((BATCH, CH, TOK), F32),
             pltpu.VMEM((HEADS, TOK, 2 * TOK), BF16),
             pltpu.VMEM((HEADS, CH, TOK), F32),
-            pltpu.VMEM((BATCH, TOK, TOK), F32),
             pltpu.VMEM((BATCH, 2 * TOK, 2 * TOK), BF16),
             dma((11,)),
             dma(()),

time: 40 us -> 39 us (0.975)
  Pallas kernels: 39.2 us -> 38 us
    pallas_call x1, Pallas kernels: 39.2 us -> 38 us  [on_device(): pl.pallas_call(kernel, out_shape=jax.ShapeDtypeStruct((ROWS, TOK), BF16),...]
where the time goes in v3:
time: 39 us; the launch traced here: 38.7 us
  Pallas kernels  38 us (97%)
  local copies, waits for them, and re-layouts  0.71 us (2%)
    pallas_call x1, Pallas kernels, on_device(): pl.pallas_call(kernel, out_shape=jax.ShapeDtypeStruct((ROWS, TOK), BF16),...  38 us

profile of v3, /device:TPU:1, one launch (start us, length us, event | category | flops | bytes accessed | tf_op | source)
XLA Modules:
  0.0 38.7 jit_solution(2458589351801517986)
XLA Ops:
  0.0 38.0 %shard_map.118 = bf16[1024,128]{1,0:T(8,128)(2,1)S(1)} custom-call(bf16[1024,128]{1,0:T(8,128)(2,1)} %skip_hbm.1, bf16[1024,128]{1,0:T(8,128)(2,1)} %r_hbm.1, bf16[1024,128]{1,0:T(8,128)(2,1)} %k_hbm.1, bf16[1024,128]{1,0:T(8,128)(2,1)} %v_hbm.1, bf16[1024,128]{1,0:T(8,128)(2,1)} %g_hbm.1, bf16[1024,128]{1,0:T(8,128)(2,1)} %w_hbm.1, ...), custom_call_target="tpu_custom_call" | custom-call | tf_op jit(solution)/shard_map/pallas_call | solution.py:494
  38.0 0.7 %copy.14 = bf16[1024,128]{1,0:T(8,128)(2,1)} copy(bf16[1024,128]{1,0:T(8,128)(2,1)S(1)} %shard_map.118) | data formatting | bytes 524288

commit v4 on v3

--- a/solution.py
+++ b/solution.py
@@ -14,6 +14,7 @@
 ROWS = 1024
 EXTRA = 16
 GROUP = 8
+LAG = 3
 BATCH = 8
 CHUNK = 128
 F32 = jnp.float32
@@ -39,7 +40,7 @@
     skip_ref, r_ref, k_ref, v_ref, g_ref, w_ref, a_ref, ef_ref, rc_ref, gm_ref, gb_ref,
     par, comb, read, local, inbox, prefix, outbox, entering, mixed, weights,
     send_a, got_a, held_b, send_b, got_b, total,
-    pull_t, key_t, ends_t, ahead_s, pair_s, inv_s, inv, part_s, seen_s,
+    pull_t, key_t, to_end, sums, ahead_s, pair_s, inv_s, inv, part_s, seen_s,
     recv_s, decay_s, solved_s, rest, both,
     in_sem, wt_sem, comb_send, comb_recv, state_send, state_recv, rs_send, rs_recv,
 ):
@@ -93,12 +94,14 @@
     row = lax.broadcasted_iota(jnp.int32, (TOK, TOK), 0)
     col = lax.broadcasted_iota(jnp.int32, (TOK, TOK), 1)
     upto = jnp.where(row <= col, 1.0, 0.0).astype(BF16)
+    sums[...] = mm(w_ref[...], upto)
     apart = row ^ col
     near = (apart >= 2) & (apart < 16)
     zero = jnp.zeros((TOK, TOK), BF16)
     diag = lax.broadcasted_iota(jnp.int32, (CH, TOK), 0) == lax.broadcasted_iota(
         jnp.int32, (CH, TOK), 1
     )
+    twice = row[:CH] == col[:CH] % CH
     left_half = lax.broadcasted_iota(jnp.int32, (CH, TOK), 1) < CH
 
     def wide(pair):
@@ -121,11 +124,11 @@
             [jnp.concatenate([one, zero], axis=1), jnp.concatenate([zero, other], axis=1)], axis=0
         )
 
-    def group_local(base):
+    def stages(base):
         for i in range(BATCH):
             rows = slice((base + i) * CH, (base + i + 1) * CH)
             w16 = w_ref[rows, :]
-            running = mm(w16, upto)
+            running = sums[rows, :]
             kf = k_ref[rows, :].astype(F32)
             scaled = kf * par[0, rows, :]
             removal = scaled * lax.rsqrt(jnp.sum(scaled * scaled, axis=0, keepdims=True) + 1e-6)
@@ -134,87 +137,98 @@
             end = running[:, 127:128]
             back = jnp.exp(mid - running)
             at_mid = jnp.exp(mid)
-            to_end = back * jnp.exp(end - mid)
             removal_fwd = -removal * jnp.exp(running - w16.astype(F32) - mid)
             pull_t[base + i] = turned(pulled * back)
             key_t[base + i] = turned(kf * back)
-            ends_t[i, :, :TOK] = turned(pulled * to_end)
-            ends_t[i, :, TOK:] = turned(kf * to_end)
+            to_end[base + i] = jnp.sum(jnp.where(twice, jnp.exp(end - mid), 0.0), axis=0, keepdims=True)
             rem_hi, rem_lo = halves(removal_fwd)
-            ahead_s[i, :CH, :] = rem_hi
-            ahead_s[i, CH:, :] = rem_lo
-            seen_s[i, CH:, :] = removal_fwd * at_mid
-            decay_s[i] = jnp.where(diag, jnp.exp(end), 0.0)
-        for i in range(BATCH):
-            ahead = ahead_s[i]
+            ahead_s[base + i, :CH, :] = rem_hi
+            ahead_s[base + i, CH:, :] = rem_lo
+            seen_s[base + i, CH:, :] = removal_fwd * at_mid
+            decay_s[base + i] = jnp.where(diag, jnp.exp(end), 0.0)
+        yield
+        for i in range(BATCH):
+            ahead = ahead_s[base + i]
             ahead = jnp.concatenate([ahead[:CH], ahead[:CH], ahead[CH:], ahead[CH:]], axis=0)
             pull = pull_t[base + i]
             from_pull = mm(jnp.concatenate([pull, pull], axis=1), ahead)
             pair_mix = jnp.where(row < col, from_pull, 0.0)
-            pair_s[i] = beside(jnp.where(apart >= 16, pair_mix, 0.0))
-            inv[i] = jnp.where(apart < 16, pair_mix, 0.0)
-            both[i, TOK:, :TOK] = jnp.where(apart == 1, pair_mix, 0.0).astype(BF16)
-            both[i, :TOK, :TOK] = jnp.where(near, pair_mix, 0.0).astype(BF16)
+            pair_s[base + i] = beside(jnp.where(apart >= 16, pair_mix, 0.0))
+            inv[base + i] = jnp.where(apart < 16, pair_mix, 0.0)
+            both[base + i, TOK:, :TOK] = jnp.where(apart == 1, pair_mix, 0.0).astype(BF16)
+            both[base + i, :TOK, :TOK] = jnp.where(near, pair_mix, 0.0).astype(BF16)
             key = key_t[base + i]
             from_key = mm(jnp.concatenate([key, key], axis=1), ahead)
-            part_s[i] = beside(jnp.where(row < col, from_key, 0.0))
+            part_s[base + i] = beside(jnp.where(row < col, from_key, 0.0))
+        yield
         for i in range(BATCH):
             rows = slice((base + i) * CH, (base + i + 1) * CH)
-            seen_s[i, :CH, :] = fold(mm(v_ref[rows, :], part_s[i]))
+            seen_s[base + i, :CH, :] = fold(mm(v_ref[rows, :], part_s[base + i]))
+        yield
         for i in range(0, BATCH, 2):
             res = mm(
-                jnp.concatenate([both[i, :TOK, :TOK], both[i + 1, :TOK, :TOK]], axis=1),
-                two_diag(both[i, TOK:, :TOK], both[i + 1, TOK:, :TOK]),
+                jnp.concatenate([both[base + i, :TOK, :TOK], both[base + i + 1, :TOK, :TOK]], axis=1),
+                two_diag(both[base + i, TOK:, :TOK], both[base + i + 1, TOK:, :TOK]),
             )
             for n in range(2):
                 more = res[:, n * TOK : (n + 1) * TOK]
-                both[i + n, :TOK, :TOK] = (both[i + n, :TOK, :TOK].astype(F32) + more).astype(BF16)
-                inv[i + n] = inv[i + n] + more
-        for _ in range(2):
+                both[base + i + n, :TOK, :TOK] = (both[base + i + n, :TOK, :TOK].astype(F32) + more).astype(BF16)
+                inv[base + i + n] = inv[base + i + n] + more
+        yield
+        for turn in range(2):
+            if turn:
+                yield
             for i in range(0, BATCH, 2):
                 res = mm(
-                    jnp.concatenate([both[i, :, :TOK], both[i + 1, :, :TOK]], axis=1),
-                    two_diag(both[i, :TOK, :TOK], both[i + 1, :TOK, :TOK]),
+                    jnp.concatenate([both[base + i, :, :TOK], both[base + i + 1, :, :TOK]], axis=1),
+                    two_diag(both[base + i, :TOK, :TOK], both[base + i + 1, :TOK, :TOK]),
                 )
                 for n in range(2):
                     e = res[:TOK, n * TOK : (n + 1) * TOK]
-                    m = inv[i + n] + res[TOK:, n * TOK : (n + 1) * TOK]
-                    both[i + n, :TOK, :TOK] = e.astype(BF16)
-                    both[i + n, TOK:, :TOK] = m.astype(BF16)
-                    inv[i + n] = m + e
+                    m = inv[base + i + n] + res[TOK:, n * TOK : (n + 1) * TOK]
+                    both[base + i + n, :TOK, :TOK] = e.astype(BF16)
+                    both[base + i + n, TOK:, :TOK] = m.astype(BF16)
+                    inv[base + i + n] = m + e
+        yield
         for i in range(0, BATCH, 2):
             res = mm(
-                jnp.concatenate([both[i, TOK:, :TOK], both[i + 1, TOK:, :TOK]], axis=1),
-                two_diag(both[i, :TOK, :TOK], both[i + 1, :TOK, :TOK]),
+                jnp.concatenate([both[base + i, TOK:, :TOK], both[base + i + 1, TOK:, :TOK]], axis=1),
+                two_diag(both[base + i, :TOK, :TOK], both[base + i + 1, :TOK, :TOK]),
             )
             for n in range(2):
-                whole = jnp.where(row == col, 1.0, inv[i + n] + res[:, n * TOK : (n + 1) * TOK])
-                inv_s[i + n] = beside(whole)
-        for i in range(BATCH):
-            left = jnp.concatenate([pair_s[i], beside(seen_s[i])], axis=0)
-            res = fold(mm(left, wide(inv_s[i])))
-            both[i] = beside(res)
-            inv[i] = res[TOK:]
-        for _ in range(2):
+                whole = jnp.where(row == col, 1.0, inv[base + i + n] + res[:, n * TOK : (n + 1) * TOK])
+                inv_s[base + i + n] = beside(whole)
+        yield
+        for i in range(BATCH):
+            left = jnp.concatenate([pair_s[base + i], beside(seen_s[base + i])], axis=0)
+            res = fold(mm(left, wide(inv_s[base + i])))
+            both[base + i] = beside(res)
+            inv[base + i] = res[TOK:]
+        yield
+        for turn in range(2):
+            if turn:
+                yield
             for i in range(BATCH):
-                res = fold(mm(both[i], wide(both[i, :TOK, :])))
-                g = inv[i] + res[TOK:]
-                both[i, :TOK, :] = beside(res[:TOK])
-                both[i, TOK:, :] = beside(g)
-                inv[i] = g
+                res = fold(mm(both[base + i], wide(both[base + i, :TOK, :])))
+                g = inv[base + i] + res[TOK:]
+                both[base + i, :TOK, :] = beside(res[:TOK])
+                both[base + i, TOK:, :] = beside(g)
+                inv[base + i] = g
+        yield
         for i in range(BATCH):
             solved_s[base + i] = beside(
-                inv[i] + fold(mm(both[i, TOK:, :], wide(both[i, :TOK, :])))
+                inv[base + i] + fold(mm(both[base + i, TOK:, :], wide(both[base + i, :TOK, :])))
             )
+        yield
         for i in range(BATCH):
             h = base + i
             rows = slice(h * CH, (h + 1) * CH)
-            pull_end = ends_t[i, :, :TOK]
-            ops = mm(solved_s[h], jnp.concatenate([pull_end, pull_end], axis=0))
-            state = ops[:CH] + mm(v_ref[rows, :], ends_t[i, :, TOK:])
+            pull = pull_t[h]
+            ops = mm(solved_s[h], jnp.concatenate([pull, pull], axis=0))
+            state = ops[:CH] + mm(v_ref[rows, :], key_t[h])
             trans = ops[CH:]
-            state = state + pltpu.roll(state, CH, 1)
-            trans = trans + pltpu.roll(trans, CH, 1) + decay_s[i]
+            state = (state + pltpu.roll(state, CH, 1)) * to_end[base + i]
+            trans = (trans + pltpu.roll(trans, CH, 1)) * to_end[base + i] + decay_s[base + i]
             sent = jnp.where(left_half, trans, state).astype(BF16)
             comb[h, :CH, :] = sent
             missed = jnp.where(diag, trans - sent.astype(F32), 0.0)
@@ -226,7 +240,7 @@
         for i in range(BATCH):
             h = base + i
             rows = slice(h * CH, (h + 1) * CH)
-            running = mm(w_ref[rows, :], upto)
+            running = sums[rows, :]
             mid = running[:, 63:64]
             recept_fwd = r_ref[rows, :].astype(F32) * jnp.exp(running - mid)
             recv_s[i] = recept_fwd * jnp.exp(mid)
@@ -272,11 +286,20 @@
 
         return carry
 
-    for base in range(0, HEADS, BATCH):
-        group_local(base)
-        if base == 0:
-            pl.semaphore_wait(barrier, SLABS - 1 + 3)
-        lax.fori_loop(base, base + BATCH, send_comb, 0)
+    ahead_of, behind = stages(0), stages(BATCH)
+    for _ in range(LAG):
+        next(ahead_of)
+    running_on = True
+    while running_on:
+        running_on = next(ahead_of, True) is None
+        if running_on:
+            next(behind)
+    pl.semaphore_wait(barrier, SLABS - 1 + 3)
+    if LAG:
+        lax.fori_loop(0, BATCH, send_comb, 0)
+    for _ in behind:
+        pass
+    lax.fori_loop(BATCH if LAG else 0, HEADS, send_comb, 0)
     for copy in second:
         copy.wait()
     spread(1, rc_ref)
@@ -517,18 +540,19 @@
             pltpu.VMEM((ROWS, TOK), F32),
             pltpu.VMEM((HEADS, TOK, TOK), BF16),
             pltpu.VMEM((HEADS, TOK, TOK), BF16),
-            pltpu.VMEM((BATCH, TOK, 2 * TOK), BF16),
-            pltpu.VMEM((BATCH, TOK, TOK), BF16),
-            pltpu.VMEM((BATCH, TOK, 2 * TOK), BF16),
-            pltpu.VMEM((BATCH, TOK, 2 * TOK), BF16),
-            pltpu.VMEM((BATCH, TOK, TOK), F32),
-            pltpu.VMEM((BATCH, TOK, 2 * TOK), BF16),
-            pltpu.VMEM((BATCH, TOK, TOK), F32),
-            pltpu.VMEM((BATCH, CH, TOK), F32),
-            pltpu.VMEM((BATCH, CH, TOK), F32),
+            pltpu.VMEM((HEADS, 1, TOK), F32),
+            pltpu.VMEM((ROWS, TOK), F32),
+            pltpu.VMEM((HEADS, TOK, TOK), BF16),
+            pltpu.VMEM((HEADS, TOK, 2 * TOK), BF16),
+            pltpu.VMEM((HEADS, TOK, 2 * TOK), BF16),
+            pltpu.VMEM((HEADS, TOK, TOK), F32),
+            pltpu.VMEM((HEADS, TOK, 2 * TOK), BF16),
+            pltpu.VMEM((HEADS, TOK, TOK), F32),
+            pltpu.VMEM((HEADS, CH, TOK), F32),
+            pltpu.VMEM((HEADS, CH, TOK), F32),
             pltpu.VMEM((HEADS, TOK, 2 * TOK), BF16),
             pltpu.VMEM((HEADS, CH, TOK), F32),
-            pltpu.VMEM((BATCH, 2 * TOK, 2 * TOK), BF16),
+            pltpu.VMEM((HEADS, 2 * TOK, 2 * TOK), BF16),
             dma((11,)),
             dma(()),
             dma((HEADS,)),

time: 39 us -> 38 us (0.974)
  Pallas kernels: 38 us -> 37 us
    pallas_call x1, Pallas kernels: 38 us -> 37 us  [on_device(): pl.pallas_call(kernel, out_shape=jax.ShapeDtypeStruct((ROWS, TOK), BF16),...]
where the time goes in v4:
time: 38 us; the launch traced here: 37.7 us
  Pallas kernels  37 us (97%)
  local copies, waits for them, and re-layouts  0.71 us (2%)
    pallas_call x1, Pallas kernels, on_device(): pl.pallas_call(kernel, out_shape=jax.ShapeDtypeStruct((ROWS, TOK), BF16),...  37 us

profile of v4, /device:TPU:1, one launch (start us, length us, event | category | flops | bytes accessed | tf_op | source)
XLA Modules:
  0.0 37.7 jit_solution(10388831084243870844)
XLA Ops:
  0.0 37.0 %shard_map.118 = bf16[1024,128]{1,0:T(8,128)(2,1)S(1)} custom-call(bf16[1024,128]{1,0:T(8,128)(2,1)} %skip_hbm.1, bf16[1024,128]{1,0:T(8,128)(2,1)} %r_hbm.1, bf16[1024,128]{1,0:T(8,128)(2,1)} %k_hbm.1, bf16[1024,128]{1,0:T(8,128)(2,1)} %v_hbm.1, bf16[1024,128]{1,0:T(8,128)(2,1)} %g_hbm.1, bf16[1024,128]{1,0:T(8,128)(2,1)} %w_hbm.1, ...), custom_call_target="tpu_custom_call" | custom-call | tf_op jit(solution)/shard_map/pallas_call | solution.py:517
  37.0 0.7 %copy.14 = bf16[1024,128]{1,0:T(8,128)(2,1)} copy(bf16[1024,128]{1,0:T(8,128)(2,1)S(1)} %shard_map.118) | data formatting | bytes 524288

commit v5 on v4

--- a/solution.py
+++ b/solution.py
@@ -60,18 +60,21 @@
     first = [pltpu.make_async_copy(*pair, in_sem.at[n]) for n, pair in enumerate(first)]
     second = [pltpu.make_async_copy(*pair, in_sem.at[6 + n]) for n, pair in enumerate(second)]
     wt_copy = pltpu.make_async_copy(wt_hbm, weights, wt_sem)
+
     for copy in first:
         copy.start()
 
     barrier = pltpu.get_barrier_semaphore()
 
-    def greet(d, carry):
-        pl.semaphore_signal(
-            barrier, inc=1, device_id=(head, lax.rem(me + d, SLABS)), device_id_type=MESH
-        )
-        return carry
-
-    lax.fori_loop(1, SLABS, greet, 0)
+    for _, dy, dx, dz in sorted(
+        (-min(dy, 4 - dy) - min(dx, 4 - dx) - dz, dy, dx, dz)
+        for dy in range(4)
+        for dx in range(4)
+        for dz in range(2)
+        if dy + dx + dz
+    ):
+        seat = (me // 8 + dy) % 4 * 8 + (me // 2 + dx) % 4 * 2 + (me + dz) % 2
+        pl.semaphore_signal(barrier, inc=1, device_id=(head, seat), device_id_type=MESH)
 
     def greet_head(d, carry):
         pl.semaphore_signal(

time: 38 us -> 38 us (level)
  no operation moved by 1% of the time
where the time goes in v5:
time: 38 us; the launch traced here: 37.7 us
  Pallas kernels  37 us (97%)
  local copies, waits for them, and re-layouts  0.71 us (2%)
    pallas_call x1, Pallas kernels, on_device(): pl.pallas_call(kernel, out_shape=jax.ShapeDtypeStruct((ROWS, TOK), BF16),...  37 us

profile of v5, /device:TPU:1, one launch (start us, length us, event | category | flops | bytes accessed | tf_op | source)
XLA Modules:
  0.0 37.7 jit_solution(13207191171319463223)
XLA Ops:
  0.0 37.0 %shard_map.118 = bf16[1024,128]{1,0:T(8,128)(2,1)S(1)} custom-call(bf16[1024,128]{1,0:T(8,128)(2,1)} %skip_hbm.1, bf16[1024,128]{1,0:T(8,128)(2,1)} %r_hbm.1, bf16[1024,128]{1,0:T(8,128)(2,1)} %k_hbm.1, bf16[1024,128]{1,0:T(8,128)(2,1)} %v_hbm.1, bf16[1024,128]{1,0:T(8,128)(2,1)} %g_hbm.1, bf16[1024,128]{1,0:T(8,128)(2,1)} %w_hbm.1, ...), custom_call_target="tpu_custom_call" | custom-call | tf_op jit(solution)/shard_map/pallas_call | solution.py:520
  37.0 0.7 %copy.14 = bf16[1024,128]{1,0:T(8,128)(2,1)} copy(bf16[1024,128]{1,0:T(8,128)(2,1)S(1)} %shard_map.118) | data formatting | bytes 524288
